TPU v7x, 32 devices: a whole 2x2x4 slice. The times are simulated.
32 devices in a mesh: parts: 2 (over x), dp: 16 (over z, y, core).
Axes of the slice: x: 2, y: 2, z: 4, core: 2. Of those that a mesh axis runs over, the one named last changes fastest.
Arguments:
- train_grads: bfloat16 [16384, 4096], P(('parts', 'dp')), parts along dimension 0, may hold values from -160 to 160
- query_grads: bfloat16 [768, 4096], P(('parts', 'dp')), parts along dimension 0, may hold values from -0.29882812 to 0.29882812
- in_basis: bfloat16 [4, 32, 32], replicated, may hold values from -1 to 1
- out_basis: bfloat16 [4, 32, 32], replicated, may hold values from -1 to 1
- damping: float32 [2], replicated, may hold values from 0.05 to 1
- layer_group: int32 [4], replicated, may hold values from 0 to 1, as said below
Outputs:
- scores: float32 [16384, 384], P(('parts', 'dp')), parts along dimension 0
There are 2 independent parts, one for each index of `parts`. A program takes and returns all parts, laid end to end along the dimension named above; an argument that names none is the same for every part. Nothing has to cross between parts.
Inputs may be any that keep to these rules, and one draw needn't show every extreme that they name: `layer_group`: every group holds at least one layer.
All inputs are finite; a program needn't handle non-finite values.
Results may differ from a plain program's by a relative error of at most 0.0065.
Values may be sent and summed in bfloat16 or wider, within the bound.
No kernel may reach another device: no remote copies, remote signals or barrier semaphores. Data moves between devices by JAX's collectives and lax.ppermute only.
A program may use at most 128 MiB of HBM per device.

v0:
```python
import jax
import jax.numpy as jnp
from jax import lax
from jax.sharding import PartitionSpec as P


def rotate(grads, in_basis, out_basis):
    layers = in_basis.shape[0]
    width = in_basis.shape[1]
    rows = grads.shape[0]
    shaped = grads.reshape(rows, layers, width, width)
    inner = jnp.einsum(
        "tlij,ljb->tlib", shaped, in_basis, preferred_element_type=jnp.float32
    ).astype(jnp.bfloat16)
    outer = jnp.einsum("tlib,lia->tlab", inner, out_basis, preferred_element_type=jnp.float32)
    return outer.reshape(rows, layers * width * width)


def per_device(train_grads, query_grads, in_basis, out_basis, damping, layer_group):
    layers = in_basis.shape[0]
    rotated = rotate(train_grads, in_basis, out_basis)
    totals = lax.psum(jnp.sum(rotated * rotated, axis=0), "dp")
    count = train_grads.shape[0] * lax.axis_size("dp")
    corrected = (totals / count).reshape(layers, -1)
    groups = damping.shape[0]
    pick = (layer_group[:, None] == jnp.arange(groups, dtype=jnp.int32)[None, :]).astype(
        jnp.float32
    )
    per_layer = jnp.sum(pick * damping[None, :], axis=1)
    denominator = (
        corrected + per_layer[:, None] * jnp.mean(corrected, axis=1, keepdims=True)
    ).reshape(-1)
    train_rounded = rotated.astype(jnp.bfloat16)
    prepared = (
        rotate(lax.all_gather(query_grads, "dp", axis=0, tiled=True), in_basis, out_basis)
        / denominator
    ).astype(jnp.bfloat16)
    return lax.dot_general(
        train_rounded, prepared, (((1,), (1,)), ((), ())), preferred_element_type=jnp.float32
    )


def solution(mesh):
    placed = (P(("parts", "dp"), None), P(("parts", "dp"), None), P(), P(), P(), P())
    return jax.shard_map(
        per_device, mesh=mesh, in_specs=placed, out_specs=P(("parts", "dp"), None), check_vma=False
    )
```

profile of v0, /device:TPU:0, one launch (start us, length us, event | category | flops | bytes accessed | tf_op | source)
XLA Modules:
  0.0 106.7 jit_solution(9189898968604316805)
XLA Ops:
  6.5 0.0 copy-start
  6.5 0.0 all-gather.2.cloned.1.call-start
  6.5 0.7 all-gather.2.cloned.1.call-update
  7.3 6.5 %copy.32 = bf16[512,4096]{0,1:T(8,128)(2,1)} copy(bf16[512,4096]{1,0:T(8,128)(2,1)} %param.6) | data formatting | bytes 8388608 | tf_op args[0]
  13.7 0.0 copy-done
  13.7 0.0 copy-start.1
  13.7 3.5 %convert_bitcast_fusion = bf16[512,4,32,32]{0,3,2,1:T(8,128)(2,1)S(1)} fusion(bf16[512,4,32,32]{0,3,2,1:T(8,128)(2,1)} %bitcast.48, bf16[4,32,32]{2,1,0:T(8,128)(2,1)S(1)} %copy-done), kind=kOutput, calls=%fused_computation.8 | convolution fusion | flops 136314880 | bytes 8396800 | tf_op jit(solution)/shard_map/tlij,ljb->tlib/dot_general | solution.py:12
  17.2 0.0 copy-done.1
  17.2 0.0 copy-start.2
  17.2 0.0 copy-start.3
  17.3 4.4 %multiply_reduce_fusion = (f32[4,32,32]{2,1,0:T(8,128)S(1)}, bf16[4,512,32,32]{1,3,2,0:T(8,128)(2,1)}) fusion(bf16[4,32,32]{2,1,0:T(8,128)(2,1)S(1)} %copy-done.1, bf16[512,4,32,32]{0,3,2,1:T(8,128)(2,1)S(1)} %convert_bitcast_fusion), kind=kOutput, calls=%fused_computation | convolution fusion | flops 140505088 | bytes 8413184 | tf_op jit(solution)/shard_map/tlib,lia->tlab/dot_general | solution.py:15
  21.6 0.1 copy.40
  21.7 0.1 reduce_sum.33
  21.8 63.5 %psum.7 = f32[4096]{0:T(1024)S(1)} all-reduce(f32[4096]{0:T(1024)S(1)} %reduce_sum.33), channel_id=1, replica_groups=mesh['parts'=2,'dp'=16] {'dp'}, use_global_device_ids=true, to_apply=%region_1.0 | all-reduce | flops 4096 | bytes 32768 | tf_op jit(solution)/shard_map/psum | solution.py:22
  85.4 0.1 reduce_sum.35
  85.5 0.0 copy-done.2
  85.5 0.0 copy-done.3
  85.5 0.1 fusion.25
  85.6 0.1 broadcast_bitcast_fusion
  85.7 0.1 div.23
  85.7 0.1 copy.41
  85.8 0.0 all-gather.2.cloned.1.call-done
  85.9 3.4 %copy.36 = bf16[384,4096]{0,1:T(8,128)(2,1)S(1)} copy(bf16[384,4096]{1,0:T(8,128)(2,1)} %all-gather.2.cloned.1.call-done) | data formatting | bytes 6291456 | tf_op jit(solution)/shard_map/all_gather | solution.py:35
  89.3 2.7 %convert_bitcast_fusion.1 = bf16[384,4,32,32]{0,3,2,1:T(8,128)(2,1)} fusion(bf16[384,4,32,32]{0,3,2,1:T(8,128)(2,1)S(1)} %bitcast.49, bf16[4,32,32]{2,1,0:T(8,128)(2,1)S(1)} %copy-done), kind=kOutput, calls=%fused_computation.11 | convolution fusion | flops 102236160 | bytes 6299648 | tf_op jit(solution)/shard_map/tlij,ljb->tlib/dot_general | solution.py:12
  92.0 7.9 %fusion.13 = f32[512,384]{1,0:T(8,128)} fusion(f32[4,32,32]{1,2,0:T(8,128)S(1)} %copy.41, bf16[384,4,32,32]{0,3,2,1:T(8,128)(2,1)} %convert_bitcast_fusion.1, bf16[4,512,32,32]{1,3,2,0:T(8,128)(2,1)} %get-tuple-element.6, bf16[4,32,32]{2,1,0:T(8,128)(2,1)S(1)} %copy-done.1), kind=kOutput, calls=%fused_computation.12 | convolution fusion | flops 1714421760 | bytes 8151040 | tf_op jit(solution)/shard_map/dot_general | solution.py:38
  (4 shorter events, 0.0 us)
Async XLA Ops:
  6.5 7.2 %copy-start = (bf16[4,32,32]{2,1,0:T(8,128)(2,1)S(1)}, bf16[4,32,32]{2,1,0:T(8,128)(2,1)}, u32[]{:S(2)}) copy-start(bf16[4,32,32]{2,1,0:T(8,128)(2,1)} %param.8) | copy-start | bytes 24580
  6.5 79.3 %all-gather.2.cloned.1.call-start = ((), (), s32[]{:S(2)}) async-start(), calls=%async_computation | async-start | bytes 3342336 | tf_op jit(solution)/shard_map/all_gather | solution.py:35
  13.7 3.5 %copy-start.1 = (bf16[4,32,32]{2,1,0:T(8,128)(2,1)S(1)}, bf16[4,32,32]{2,1,0:T(8,128)(2,1)}, u32[]{:S(2)}) copy-start(bf16[4,32,32]{2,1,0:T(8,128)(2,1)} %param.9) | copy-start | bytes 24580
  17.2 68.3 %copy-start.2 = (f32[2]{0:T(128)S(1)}, f32[2]{0:T(128)}, u32[]{:S(2)}) copy-start(f32[2]{0:T(128)} %param.10) | copy-start | bytes 28
  17.2 68.2 %copy-start.3 = (s32[4]{0:T(128)S(1)}, s32[4]{0:T(128)}, u32[]{:S(2)}) copy-start(s32[4]{0:T(128)} %param.11) | copy-start | bytes 52
Sparse Core Ops, SparseCore 0:
  9.6 48.3 all-gather.1
where the time goes:
time: 107 us
  blocking collectives  63.5 us (59%)
  matrix products  18.5 us (17%)
  between operations  13.5 us (13%)
  local copies, waits for them, and re-layouts  10.3 us (10%)
    psum x1, blocking collectives, per_device(): totals = lax.psum(jnp.sum(rotated * rotated, axis=0), 'dp')  63.5 us
    dot_general x1, matrix products, per_device(): lax.dot_general(train_rounded, prepared, (((1,), (1,)), ((), ())), prefer...  7.9 us
    unnamed x10, local copies, waits for them, and re-layouts  6.57 us
    dot_general x2, matrix products, rotate(): jnp.einsum('tlij,ljb->tlib', shaped, in_basis, preferred_element_type=jnp...  6.18 us
    dot_general x1, matrix products, rotate(): jnp.einsum('tlib,lia->tlab', inner, out_basis, preferred_element_type=jnp...  4.39 us
    all_gather x1, local copies, waits for them, and re-layouts, per_device(): lax.all_gather(query_grads, 'dp', axis=0, tiled=True)  3.43 us
  transfers between devices with their start and end apart: 1, of which 0 were waited for; matrix products, arithmetic and copies ran while one was open for 14% of the time, Pallas kernels for 0%

commit v1 on v0

--- a/solution.py
+++ b/solution.py
@@ -19,7 +19,7 @@
 def per_device(train_grads, query_grads, in_basis, out_basis, damping, layer_group):
     layers = in_basis.shape[0]
     rotated = rotate(train_grads, in_basis, out_basis)
-    totals = lax.psum(jnp.sum(rotated * rotated, axis=0), "dp")
+    totals = jnp.sum(lax.all_gather(jnp.sum(rotated * rotated, axis=0), "dp"), axis=0)
     count = train_grads.shape[0] * lax.axis_size("dp")
     corrected = (totals / count).reshape(layers, -1)
     groups = damping.shape[0]

time: 107 us -> 79.3 us (0.74)
  blocking collectives: 63.5 us -> 24.3 us
  waiting for transfers between devices: 0.73 us -> 12.1 us
    psum x1 -> x0, blocking collectives: 63.5 us -> none  [per_device(): totals = lax.psum(jnp.sum(rotated * rotated, axis=0), 'dp')]
    all_gather x0 -> x1, blocking collectives: none -> 24.3 us  [per_device(): lax.all_gather(jnp.sum(rotated * rotated, axis=0), 'dp')]
    all_gather x1, waiting for transfers between devices: 0.02 us -> 11.4 us  [per_device(): lax.all_gather(query_grads, 'dp', axis=0, tiled=True)]
  transfers between devices with their start and end apart: 1 -> 1, of which waited for: 0 -> 1; matrix products, arithmetic and copies ran while one was open for 14% -> 19% of each run, Pallas kernels for 0% -> 0%
where the time goes in v1:
time: 79.3 us; the launch traced here: 79 us
  blocking collectives  24.3 us (31%)
  matrix products  18.5 us (23%)
  between operations  13.5 us (17%)
  waiting for transfers between devices  12.1 us (15%)
  local copies, waits for them, and re-layouts  10.3 us (13%)
    all_gather x1, blocking collectives, per_device(): lax.all_gather(jnp.sum(rotated * rotated, axis=0), 'dp')  24.3 us
    all_gather x1, waiting for transfers between devices, per_device(): lax.all_gather(query_grads, 'dp', axis=0, tiled=True)  11.4 us
    dot_general x1, matrix products, per_device(): lax.dot_general(train_rounded, prepared, (((1,), (1,)), ((), ())), prefer...  7.91 us
    unnamed x10, local copies, waits for them, and re-layouts  6.59 us
    dot_general x2, matrix products, rotate(): jnp.einsum('tlij,ljb->tlib', shaped, in_basis, preferred_element_type=jnp...  6.18 us
    dot_general x1, matrix products, rotate(): jnp.einsum('tlib,lia->tlab', inner, out_basis, preferred_element_type=jnp...  4.39 us
    all_gather x1, local copies, waits for them, and re-layouts, per_device(): lax.all_gather(query_grads, 'dp', axis=0, tiled=True)  3.42 us
  transfers between devices with their start and end apart: 1, of which 1 were waited for; matrix products, arithmetic and copies ran while one was open for 19% of the time, Pallas kernels for 0%

profile of v1, /device:TPU:0, one launch (start us, length us, event | category | flops | bytes accessed | tf_op | source)
XLA Modules:
  0.0 79.0 jit_solution(13597816394709548898)
XLA Ops:
  6.5 0.0 copy-start
  6.5 0.0 all-gather.3.cloned.1.call-start
  6.5 0.7 all-gather.3.cloned.1.call-update
  7.3 6.5 %copy.32 = bf16[512,4096]{0,1:T(8,128)(2,1)} copy(bf16[512,4096]{1,0:T(8,128)(2,1)} %param.6) | data formatting | bytes 8388608 | tf_op args[0]
  13.7 0.0 copy-done
  13.7 0.0 copy-start.1
  13.7 3.5 %convert_bitcast_fusion = bf16[512,4,32,32]{0,3,2,1:T(8,128)(2,1)S(1)} fusion(bf16[512,4,32,32]{0,3,2,1:T(8,128)(2,1)} %bitcast.44, bf16[4,32,32]{2,1,0:T(8,128)(2,1)S(1)} %copy-done), kind=kOutput, calls=%fused_computation.8 | convolution fusion | flops 136314880 | bytes 8396800 | tf_op jit(solution)/shard_map/tlij,ljb->tlib/dot_general | solution.py:12
  17.2 0.0 copy-done.1
  17.2 0.0 copy-start.2
  17.2 0.0 copy-start.3
  17.3 4.4 %multiply_reduce_fusion = (f32[4,32,32]{2,1,0:T(8,128)S(1)}, bf16[4,512,32,32]{1,3,2,0:T(8,128)(2,1)}) fusion(bf16[4,32,32]{2,1,0:T(8,128)(2,1)S(1)} %copy-done.1, bf16[512,4,32,32]{0,3,2,1:T(8,128)(2,1)S(1)} %convert_bitcast_fusion), kind=kOutput, calls=%fused_computation | convolution fusion | flops 140505088 | bytes 8413184 | tf_op jit(solution)/shard_map/tlib,lia->tlab/dot_general | solution.py:15
  21.6 0.1 copy.40
  21.7 0.1 reshape.48
  21.8 24.3 %all-gather = f32[16,1,4096]{2,1,0:T(1,128)S(1)} all-gather(f32[1,1,4096]{2,1,0:T(1,128)S(1)} %reshape.48), channel_id=1, replica_groups=mesh['parts'=2,'dp'=16] {'dp'}, dimensions={0}, use_global_device_ids=true | all-gather | bytes 278528 | tf_op jit(solution)/shard_map/all_gather | solution.py:22
  46.1 0.2 reduce_sum.40
  46.3 0.1 div.24
  46.4 0.1 reduce_sum.42
  46.5 0.0 copy-done.2
  46.5 0.0 copy-done.3
  46.5 0.1 fusion.25
  46.6 0.1 broadcast_add_fusion
  46.7 0.1 copy.41
  46.8 11.4 %all-gather.3.cloned.1.call-done = bf16[384,4096]{1,0:T(8,128)(2,1)} async-done(((bf16[24,4096]{1,0:T(8,128)(2,1)}), bf16[384,4096]{1,0:T(8,128)(2,1)}) %all-gather.3.cloned.1.call-update) | async-done | bytes 3145744 | tf_op jit(solution)/shard_map/all_gather | solution.py:35
  58.1 3.4 %copy.36 = bf16[384,4096]{0,1:T(8,128)(2,1)S(1)} copy(bf16[384,4096]{1,0:T(8,128)(2,1)} %all-gather.3.cloned.1.call-done) | data formatting | bytes 6291456 | tf_op jit(solution)/shard_map/all_gather | solution.py:35
  61.6 2.7 %convert_bitcast_fusion.1 = bf16[384,4,32,32]{0,3,2,1:T(8,128)(2,1)} fusion(bf16[384,4,32,32]{0,3,2,1:T(8,128)(2,1)S(1)} %bitcast.45, bf16[4,32,32]{2,1,0:T(8,128)(2,1)S(1)} %copy-done), kind=kOutput, calls=%fused_computation.11 | convolution fusion | flops 102236160 | bytes 6299648 | tf_op jit(solution)/shard_map/tlij,ljb->tlib/dot_general | solution.py:12
  64.3 7.9 %fusion.13 = f32[512,384]{1,0:T(8,128)} fusion(f32[4,32,32]{1,2,0:T(8,128)S(1)} %copy.41, bf16[384,4,32,32]{0,3,2,1:T(8,128)(2,1)} %convert_bitcast_fusion.1, bf16[4,512,32,32]{1,3,2,0:T(8,128)(2,1)} %get-tuple-element.6, bf16[4,32,32]{2,1,0:T(8,128)(2,1)S(1)} %copy-done.1), kind=kOutput, calls=%fused_computation.12 | convolution fusion | flops 1714421760 | bytes 8151040 | tf_op jit(solution)/shard_map/dot_general | solution.py:38
  (3 shorter events, 0.0 us)
Async XLA Ops:
  6.5 7.2 %copy-start = (bf16[4,32,32]{2,1,0:T(8,128)(2,1)S(1)}, bf16[4,32,32]{2,1,0:T(8,128)(2,1)}, u32[]{:S(2)}) copy-start(bf16[4,32,32]{2,1,0:T(8,128)(2,1)} %param.8) | copy-start | bytes 24580
  6.5 51.6 %all-gather.3.cloned.1.call-start = ((), (), s32[]{:S(2)}) async-start(), calls=%async_computation | async-start | bytes 3342336 | tf_op jit(solution)/shard_map/all_gather | solution.py:35
  13.7 3.5 %copy-start.1 = (bf16[4,32,32]{2,1,0:T(8,128)(2,1)S(1)}, bf16[4,32,32]{2,1,0:T(8,128)(2,1)}, u32[]{:S(2)}) copy-start(bf16[4,32,32]{2,1,0:T(8,128)(2,1)} %param.9) | copy-start | bytes 24580
  17.2 29.3 %copy-start.2 = (f32[2]{0:T(128)S(1)}, f32[2]{0:T(128)}, u32[]{:S(2)}) copy-start(f32[2]{0:T(128)} %param.10) | copy-start | bytes 28
  17.2 29.3 %copy-start.3 = (s32[4]{0:T(128)S(1)}, s32[4]{0:T(128)}, u32[]{:S(2)}) copy-start(s32[4]{0:T(128)} %param.11) | copy-start | bytes 52
Sparse Core Ops, SparseCore 0:
  9.6 48.4 all-gather.2
